TPU v7x, 32 devices: a whole 2x2x4 slice. The times are simulated.
32 devices in a mesh: dp: 4 (over z), mp: 8 (over y, x, core).
Axes of the slice: x: 2, y: 2, z: 4, core: 2. Of those that a mesh axis runs over, the one named last changes fastest.
Arguments:
- tokens: bfloat16 [4096, 4096], P('dp', 'mp'), may hold values from -6 to 6
- decay: float32 [4096, 16], P('dp'), may hold values from 0.75 to 1, as said below
- state: float32 [128, 256, 8192], P('dp', None, 'mp'), may hold values from -24 to 24
- w_query: bfloat16 [4096, 4096], P(None, 'mp'), may hold values from -0.09375 to 0.09375
- w_key: bfloat16 [4096, 4096], P(None, 'mp'), may hold values from -0.09375 to 0.09375
- w_value: bfloat16 [4096, 8192], P(None, 'mp'), may hold values from -0.09375 to 0.09375
- w_gate: bfloat16 [4096, 8192], P(None, 'mp'), may hold values from -0.09375 to 0.09375
- w_out: bfloat16 [8192, 4096], P('mp'), may hold values from -0.09375 to 0.09375
- norm_gain: float32 [8192], P('mp'), may hold values from 0.25 to 1.75
Outputs:
- layer_out: bfloat16 [4096, 4096], P('dp', 'mp')
- new_state: float32 [128, 256, 8192], P('dp', None, 'mp')
Inputs may be any that keep to these rules, and one draw needn't show every extreme that they name: `decay`: each head has its own base rate over all tokens, varied somewhat from token to token.
All inputs are finite; a program needn't handle non-finite values.
Results may differ from a plain program's by a relative error of at most 0.0071.
Values may be sent and summed in bfloat16 or wider, within the bound.
A program may use at most 256 MiB of HBM per device.

v0:
```python
import functools

import jax
import jax.numpy as jnp
from jax import lax
from jax.experimental import pallas as pl
from jax.experimental.pallas import tpu as pltpu
from jax.sharding import PartitionSpec as P

HEAD = 256
VHEAD = 512
NEW = 32


EPS = 0.1


def partner(shard, axis, bit):
    return lax.ppermute(shard, axis, [(i, i ^ 1 << bit) for i in range(lax.axis_size(axis))])


def split_heads(tokens, decay, state, w_query, w_key, w_value, w_gate, w_out, norm_gain):
    highest = lax.Precision.HIGHEST
    tok_rows = tokens.shape[0]
    qk_columns = w_query.shape[1]
    v_columns = w_value.shape[1]
    head_span = max(1, HEAD // qk_columns)
    groups = max(1, qk_columns // HEAD)
    qk_width = qk_columns // groups
    v_width = v_columns // groups
    sequences = tok_rows // NEW
    bit_count = head_span.bit_length() - 1
    device_index = lax.axis_index("mp")
    first_head = device_index * qk_columns // HEAD
    qk_zeros = jnp.zeros((tok_rows, qk_columns), jnp.float32)
    v_zeros = jnp.zeros((tok_rows, v_columns), jnp.float32)
    carried = (qk_zeros, qk_zeros, v_zeros, v_zeros)
    segment = lax.all_gather(tokens, "mp", axis=1, tiled=True)
    updated = []
    for running, weight in zip(carried, (w_query, w_key, w_value, w_gate)):
        updated.append(jnp.dot(segment, weight, preferred_element_type=jnp.float32))
    query, key_proj, value_proj, gate_proj = tuple(updated)
    query = (query * HEAD ** (-0.5)).astype(jnp.bfloat16).reshape(tok_rows, groups, qk_width)
    key_proj = key_proj.astype(jnp.bfloat16).reshape(tok_rows, groups, qk_width)
    value_proj = value_proj.astype(jnp.bfloat16)
    for bit_number in range(bit_count):
        other_query, other_key = partner((query, key_proj), "mp", bit_number)
        upper_half = device_index >> bit_number & 1 == 1
        query = jnp.where(
            upper_half,
            jnp.concatenate([other_query, query], 2),
            jnp.concatenate([query, other_query], 2),
        )
        key_proj = jnp.where(
            upper_half,
            jnp.concatenate([other_key, key_proj], 2),
            jnp.concatenate([key_proj, other_key], 2),
        )
    query_block = query.reshape(sequences, NEW, groups, HEAD)
    key_block = key_proj.reshape(sequences, NEW, groups, HEAD)
    value_block = value_proj.reshape(sequences, NEW, groups, v_width)
    decay_rates = lax.dynamic_slice_in_dim(decay, first_head, groups, 1).reshape(
        sequences, NEW, groups
    )
    log_cumul = jnp.cumsum(jnp.log(decay_rates), axis=1)
    old_state = state.reshape(sequences, HEAD, groups, v_width)
    from_state = jnp.einsum(
        "bngk,bkgv->bngv", query_block.astype(jnp.float32), old_state, precision=highest
    )
    scores = jnp.einsum(
        "bngk,bmgk->bgnm", query_block, key_block, preferred_element_type=jnp.float32
    )
    along = jnp.transpose(log_cumul, (0, 2, 1))
    log_gap = along[:, :, :, None] - along[:, :, None, :]
    causal = jnp.arange(NEW)[:, None] >= jnp.arange(NEW)[None, :]
    factor = jnp.where(causal, jnp.exp(jnp.where(causal, log_gap, 0.0)), 0.0)
    weights = (scores * factor).astype(jnp.bfloat16)
    in_block = jnp.einsum(
        "bgnm,bmgv->bngv", weights, value_block, preferred_element_type=jnp.float32
    )
    retained = jnp.exp(log_cumul)[..., None] * from_state + in_block
    final_log = log_cumul[:, -1, :]
    carry_scale = jnp.exp(final_log[:, None, :] - log_cumul)
    decayed_keys = key_block.astype(jnp.float32) * carry_scale[..., None]
    fresh = jnp.einsum(
        "bngk,bngv->bkgv", decayed_keys, value_block.astype(jnp.float32), precision=highest
    )
    new_state = jnp.exp(final_log)[:, None, :, None] * old_state + fresh
    new_state = new_state.reshape(sequences, HEAD, v_columns)
    retained = retained.reshape(tok_rows, groups, v_width)
    running = jnp.sum(retained, axis=-1)
    squares = jnp.sum(retained * retained, axis=-1)
    for bit_number in range(bit_count):
        other_sum, other_square = partner((running, squares), "mp", bit_number)
        running = running + other_sum
        squares = squares + other_square
    centre = running / VHEAD
    variance = squares / VHEAD - centre * centre
    deviation = retained - centre[..., None]
    normed = deviation * lax.rsqrt(variance + EPS)[..., None]
    gated_out = (normed.reshape(tok_rows, v_columns) * norm_gain * jax.nn.silu(gate_proj)).astype(
        jnp.bfloat16
    )
    partial_terms = jnp.dot(gated_out, w_out, preferred_element_type=jnp.float32)
    layer_out = lax.psum_scatter(partial_terms, "mp", scatter_dimension=1, tiled=True).astype(
        jnp.bfloat16
    )
    return (layer_out, new_state)


CHUNKS = 4
PER_STEP = 2
TILE = 512


def retention_step(
    per_step, groups, c_col, c_row, q, k, v, gate, gain, state, *rest
):
    gated, new_state = rest[-2:]
    vw = v.shape[1] // groups
    rows = lax.broadcasted_iota(jnp.int32, (NEW, NEW), 0)
    cols = lax.broadcasted_iota(jnp.int32, (NEW, NEW), 1)
    causal = rows >= cols
    for s in range(per_step):
        at = slice(s * NEW, (s + 1) * NEW)
        for g in range(groups):
            vs = slice(g * vw, (g + 1) * vw)
            ks = slice(g * HEAD, (g + 1) * HEAD)
            col = c_col[at, g : g + 1]
            row = c_row[s, g : g + 1, :]
            last = col[NEW - 1 : NEW, :]
            factor = jnp.where(causal, jnp.exp(jnp.where(causal, col - row, 0.0)), 0.0)
            query, key, value = q[at, ks], k[at, ks], v[at, vs]
            scores = lax.dot_general(
                query, key, (((1,), (1,)), ((), ())), preferred_element_type=jnp.float32
            )
            weights = (scores * factor).astype(jnp.bfloat16)
            old = state[s, :, vs]
            from_state = jnp.dot(
                query, old.astype(jnp.bfloat16), preferred_element_type=jnp.float32
            )
            in_block = jnp.dot(weights, value, preferred_element_type=jnp.float32)
            retained = jnp.exp(col) * from_state + in_block
            scaled = (key.astype(jnp.float32) * jnp.exp(last - col)).astype(jnp.bfloat16)
            fresh = lax.dot_general(
                scaled, value, (((0,), (0,)), ((), ())), preferred_element_type=jnp.float32
            )
            new_state[s, :, vs] = jnp.exp(last) * old + fresh
            centre = jnp.mean(retained, axis=1, keepdims=True)
            deviation = retained - centre
            variance = jnp.mean(deviation * deviation, axis=1, keepdims=True)
            normed = deviation * lax.rsqrt(variance + EPS)
            gates = gate[at, vs]
            silu = gates / (1.0 + jnp.exp(-gates))
            gated[at, vs] = (normed * gain[:, vs] * silu).astype(jnp.bfloat16)


def retention(chunk, chunks, c_col, c_row, q, k, v, gate, gain, state, previous):
    rows, groups = c_col.shape
    sequences = rows // NEW
    per_step = PER_STEP if sequences % PER_STEP == 0 else 1
    steps = sequences // per_step
    step_rows = per_step * NEW
    qk, vc = q.shape[1], v.shape[1]
    first = chunk * steps
    by_row = lambda width: pl.BlockSpec((step_rows, width), lambda i: (i, 0))
    state_spec = pl.BlockSpec((per_step, HEAD, vc), lambda i: (first + i, 0, 0))
    in_specs = [
        by_row(groups),
        pl.BlockSpec((per_step, groups, NEW), lambda i: (i, 0, 0)),
        by_row(qk),
        by_row(qk),
        by_row(vc),
        by_row(vc),
        pl.BlockSpec((1, vc), lambda i: (0, 0)),
        state_spec,
    ]
    operands = [c_col, c_row, q, k, v, gate, gain, state]
    aliases = {}
    if previous is not None:
        in_specs.append(pl.BlockSpec(memory_space=pl.ANY))
        aliases = {len(operands): 1}
        operands.append(previous)
    return pl.pallas_call(
        functools.partial(retention_step, per_step, groups),
        grid=(steps,),
        in_specs=in_specs,
        out_specs=[by_row(vc), state_spec],
        out_shape=[
            jax.ShapeDtypeStruct((rows, vc), jnp.bfloat16),
            jax.ShapeDtypeStruct(state.shape, jnp.float32),
        ],
        input_output_aliases=aliases,
        compiler_params=pltpu.CompilerParams(
            dimension_semantics=("arbitrary",), vmem_limit_bytes=40 << 20
        ),
        cost_estimate=pl.CostEstimate(
            flops=12 * rows * HEAD * vc,
            bytes_accessed=8 * sequences * HEAD * vc,
            transcendentals=rows * vc,
        ),
    )(*operands)


def partners(device):
    core = device % 2
    across_x = device + 2 - 4 * ((device // 2) % 2)
    across_y = device + 4 - 8 * (device // 4)
    near = across_x + core * (across_y - across_x)
    far = across_y + core * (across_x - across_y)
    return near, far, across_x + across_y - device, device + 1 - 2 * core


def meet(devices):
    barrier = pltpu.get_barrier_semaphore()
    for device in devices:
        pl.semaphore_signal(
            barrier, inc=1, device_id={"mp": device}, device_id_type=pl.DeviceIdType.MESH
        )
    pl.semaphore_wait(barrier, len(devices))


def remote(source, target, send, recv, device):
    return pltpu.make_async_remote_copy(
        src_ref=source,
        dst_ref=target,
        send_sem=send,
        recv_sem=recv,
        device_id={"mp": device},
        device_id_type=pl.DeviceIdType.MESH,
    )


def project_kernel(
    chunks,
    tokens,
    w_query,
    w_key,
    w_value,
    w_gate,
    query,
    key_proj,
    value_proj,
    gate_proj,
    gathered,
    wq,
    wk,
    wv,
    wg,
    q_held,
    k_held,
    v_held,
    g_held,
    load_sem,
    out_sem,
    send,
    recv,
):
    me = lax.axis_index("mp")
    near, far, diagonal, sibling = partners(me)
    sib_near, sib_far, sib_diagonal, _ = partners(sibling)
    rows, width = tokens.shape
    size = rows // chunks

    def block(device, r):
        return gathered.at[
            pl.ds(pl.multiple_of(r * size, size), size),
            pl.ds(pl.multiple_of(device * width, width), width),
        ]

    def copy(lane, source, target, r):
        there = block(source, r)
        return remote(there, there, send.at[lane, r], recv.at[lane, r], target)

    own = pltpu.make_async_copy(
        tokens, gathered.at[:, pl.ds(pl.multiple_of(me * width, width), width)], load_sem.at[0]
    )
    own.start()
    loads = [
        pltpu.make_async_copy(source, held, load_sem.at[1 + n])
        for n, (source, held) in enumerate(
            ((w_query, wq), (w_key, wk), (w_value, wv), (w_gate, wg))
        )
    ]
    for load in loads:
        load.start()
    meet((near, far, sibling))
    own.wait()
    for r in range(chunks):
        copy(0, me, near, r).start()
        if r == 0:
            copy(1, me, far, r).start()
        copy(3, me, sibling, r).start()

    def forward(r):
        copy(0, near, near, r).wait_recv()
        copy(2, near, far, r).start()
        copy(4, near, sibling, r).start()

        @pl.when(r + 1 < chunks)
        def _():
            copy(1, me, far, r + 1).start()

    def project(r, held, weight, scale, out, n):
        at = pl.ds(pl.multiple_of(r * size, size), size)
        for col in range(0, weight.shape[1], TILE):
            cols = slice(col, min(col + TILE, weight.shape[1]))
            part = jnp.dot(gathered[at, :], weight[:, cols], preferred_element_type=jnp.float32)
            if scale is not None:
                part = part * scale
            held[at, cols] = part.astype(held.dtype)
        pltpu.make_async_copy(held.at[at, :], out.at[at, :], out_sem.at[n, r]).start()

    sets = (
        (q_held, wq, HEAD ** (-0.5), query),
        (k_held, wk, None, key_proj),
        (v_held, wv, None, value_proj),
        (g_held, wg, None, gate_proj),
    )
    forward(0)

    def step(r, carry):
        copy(1, far, far, r).wait_recv()
        copy(5, far, sibling, r).start()
        copy(2, diagonal, far, r).wait_recv()
        copy(6, diagonal, sibling, r).start()

        @pl.when(r + 1 < chunks)
        def _():
            forward(r + 1)

        copy(3, sibling, sibling, r).wait_recv()
        copy(4, sib_near, sibling, r).wait_recv()
        copy(5, sib_far, sibling, r).wait_recv()
        copy(6, sib_diagonal, sibling, r).wait_recv()
        for n, (held, weight, scale, out) in enumerate(sets):

            @pl.when(r == 0)
            def _():
                loads[n].wait()

            project(r, held, weight, scale, out, n)
        return carry

    lax.fori_loop(0, chunks, step, 0)

    def drain(r, carry):
        at = pl.ds(pl.multiple_of(r * size, size), size)
        for lane, (source, target) in enumerate(
            (
                (me, near),
                (me, far),
                (near, far),
                (me, sibling),
                (near, sibling),
                (far, sibling),
                (diagonal, sibling),
            )
        ):
            copy(lane, source, target, r).wait_send()
        for n, (held, weight, scale, out) in enumerate(sets):
            pltpu.make_async_copy(held.at[at, :], out.at[at, :], out_sem.at[n, r]).wait()
        return carry

    lax.fori_loop(0, chunks, drain, 0)


def gather_project(tokens, w_query, w_key, w_value, w_gate):
    rows, width = tokens.shape
    depth, qk = w_query.shape
    vc = w_value.shape[1]
    chunks = CHUNKS
    shapes = [
        ((rows, qk), jnp.bfloat16),
        ((rows, qk), jnp.bfloat16),
        ((rows, vc), jnp.bfloat16),
        ((rows, vc), jnp.float32),
    ]
    anywhere = pl.BlockSpec(memory_space=pl.ANY)
    return pl.pallas_call(
        functools.partial(project_kernel, chunks),
        in_specs=[anywhere] * 5,
        out_specs=[anywhere] * 4,
        out_shape=[jax.ShapeDtypeStruct(*shape) for shape in shapes],
        scratch_shapes=[
            pltpu.VMEM((rows, depth), jnp.bfloat16),
            pltpu.VMEM((depth, qk), jnp.bfloat16),
            pltpu.VMEM((depth, qk), jnp.bfloat16),
            pltpu.VMEM((depth, vc), jnp.bfloat16),
            pltpu.VMEM((depth, vc), jnp.bfloat16),
        ]
        + [pltpu.VMEM(*shape) for shape in shapes]
        + [
            pltpu.SemaphoreType.DMA((5,)),
            pltpu.SemaphoreType.DMA((4, chunks)),
            pltpu.SemaphoreType.DMA((7, chunks)),
            pltpu.SemaphoreType.DMA((7, chunks)),
        ],
        compiler_params=pltpu.CompilerParams(
            collective_id=0, has_side_effects=True, vmem_limit_bytes=56 << 20
        ),
    )(tokens, w_query, w_key, w_value, w_gate)


def output_kernel(
    chunks,
    gated,
    w_out,
    layer_out,
    gated_held,
    w_held,
    to_sibling,
    from_sibling,
    outgoing,
    incoming,
    total,
    load_sem,
    send,
    recv,
):
    me = lax.axis_index("mp")
    near, far, diagonal, sibling = partners(me)
    sib_near, sib_far, sib_diagonal, _ = partners(sibling)
    width = layer_out.shape[1]
    rows = gated.shape[0]
    size = rows // chunks
    loads = [
        pltpu.make_async_copy(gated, gated_held, load_sem.at[0]),
        pltpu.make_async_copy(w_out, w_held, load_sem.at[1]),
    ]
    for load in loads:
        load.start()
    meet((near, far, sibling))
    for load in loads:
        load.wait()
    mine = (me, near, far, diagonal)
    theirs = (sibling, sib_near, sib_far, sib_diagonal)

    def at(r):
        return pl.ds(pl.multiple_of(r * size, size), size)

    def share(dest, r):
        return jnp.dot(
            gated_held[at(r), :],
            w_held[:, pl.ds(pl.multiple_of(dest * width, width), width)],
            preferred_element_type=jnp.float32,
        )

    def swap(j, r):
        return remote(
            to_sibling.at[j, at(r), :],
            from_sibling.at[j, at(r), :],
            send.at[j, r],
            recv.at[j, r],
            sibling,
        )

    def hop(lane, r):
        return remote(
            outgoing.at[lane, at(r), :],
            incoming.at[lane, at(r), :],
            send.at[4 + lane, r],
            recv.at[4 + lane, r],
            near if lane == 0 else far,
        )

    for j in (3, 2, 1, 0):

        def give(r, carry):
            to_sibling[j, at(r), :] = share(theirs[j], r).astype(jnp.bfloat16)
            swap(j, r).start()
            return carry

        def combine(r, carry):
            part = share(mine[j], r)
            swap(j, r).wait_recv()
            part = part + from_sibling[j, at(r), :].astype(jnp.float32)
            if j == 1:
                hop(2, r).wait_recv()
                part = part + incoming[2, at(r), :].astype(jnp.float32)
            if j == 0:
                total[at(r), :] = part
            else:
                outgoing[j - 1, at(r), :] = part.astype(jnp.bfloat16)
                hop(j - 1, r).start()
            return carry

        lax.fori_loop(0, chunks, give, 0)
        lax.fori_loop(0, chunks, combine, 0)

    def finish(r, carry):
        hop(1, r).wait_recv()
        hop(0, r).wait_recv()
        layer_out[at(r), :] = (
            total[at(r), :]
            + incoming[0, at(r), :].astype(jnp.float32)
            + incoming[1, at(r), :].astype(jnp.float32)
        ).astype(jnp.bfloat16)
        for j in range(4):
            swap(j, r).wait_send()
        for lane in range(3):
            hop(lane, r).wait_send()
        return carry

    lax.fori_loop(0, chunks, finish, 0)


def project_out(gated, w_out, width):
    rows = gated.shape[0]
    chunks = CHUNKS
    anywhere = pl.BlockSpec(memory_space=pl.ANY)
    return pl.pallas_call(
        functools.partial(output_kernel, chunks),
        in_specs=[anywhere] * 2,
        out_specs=pl.BlockSpec(memory_space=pltpu.VMEM),
        out_shape=jax.ShapeDtypeStruct((rows, width), jnp.bfloat16),
        scratch_shapes=[
            pltpu.VMEM(gated.shape, jnp.bfloat16),
            pltpu.VMEM(w_out.shape, jnp.bfloat16),
            pltpu.VMEM((4, rows, width), jnp.bfloat16),
            pltpu.VMEM((4, rows, width), jnp.bfloat16),
            pltpu.VMEM((3, rows, width), jnp.bfloat16),
            pltpu.VMEM((3, rows, width), jnp.bfloat16),
            pltpu.VMEM((rows, width), jnp.float32),
            pltpu.SemaphoreType.DMA((2,)),
            pltpu.SemaphoreType.DMA((7, chunks)),
            pltpu.SemaphoreType.DMA((7, chunks)),
        ],
        compiler_params=pltpu.CompilerParams(
            collective_id=1, has_side_effects=True, vmem_limit_bytes=56 << 20
        ),
    )(gated, w_out)


def whole_heads(tokens, decay, state, w_query, w_key, w_value, w_gate, w_out, norm_gain):
    tok_rows = tokens.shape[0]
    groups = w_query.shape[1] // HEAD
    sequences = tok_rows // NEW
    first_head = lax.axis_index("mp") * groups
    logs = jnp.log(lax.dynamic_slice_in_dim(decay, first_head, groups, 1))
    logs = logs.reshape(sequences, NEW, groups)
    causal = jnp.arange(NEW)[:, None] >= jnp.arange(NEW)[None, :]
    cumul = jnp.sum(jnp.where(causal[None, :, :, None], logs[:, None], 0.0), axis=2)
    c_col = cumul.reshape(tok_rows, groups)
    c_row = jnp.transpose(cumul, (0, 2, 1))
    query, key_proj, value_proj, gate_proj = gather_project(
        tokens, w_query, w_key, w_value, w_gate
    )
    gated_out, new_state = retention(
        0,
        1,
        c_col,
        c_row,
        query,
        key_proj,
        value_proj,
        gate_proj,
        norm_gain.reshape(1, -1),
        state,
        None,
    )
    return (project_out(gated_out, w_out, tokens.shape[1]), new_state)


def per_device(tokens, decay, state, w_query, *rest):
    whole = w_query.shape[1] % HEAD == 0 and lax.axis_size("mp") == 8
    path = whole_heads if whole else split_heads
    return path(tokens, decay, state, w_query, *rest)


def solution(mesh):
    placed = (
        P("dp", "mp"),
        P("dp", None),
        P("dp", None, "mp"),
        P(None, "mp"),
        P(None, "mp"),
        P(None, "mp"),
        P(None, "mp"),
        P("mp", None),
        P("mp"),
    )
    return jax.shard_map(
        per_device,
        mesh=mesh,
        in_specs=placed,
        out_specs=(P("dp", "mp"), P("dp", None, "mp")),
        check_vma=False,
    )
```

profile of v0, /device:TPU:0, one launch (start us, length us, event | category | flops | bytes accessed | tf_op | source)
XLA Modules:
  0.0 143.8 jit_solution(11396791030830854516)
XLA Ops:
  0.6 0.8 dynamic-slice_log_fusion
  1.4 0.1 broadcast_in_dim.26
  1.5 0.4 select_reduce_fusion
  1.9 0.3 copy.18
  2.2 0.0 copy-start.5
  2.2 55.7 %shard_map.104 = (bf16[1024,512]{1,0:T(8,128)(2,1)}, bf16[1024,512]{1,0:T(8,128)(2,1)}, bf16[1024,1024]{1,0:T(8,128)(2,1)}, f32[1024,1024]{1,0:T(8,128)}) custom-call(bf16[1024,512]{1,0:T(8,128)(2,1)} %tokens.1, bf16[4096,512]{1,0:T(8,128)(2,1)} %w_query.1, bf16[4096,512]{1,0:T(8,128)(2,1)} %w_key.1, bf16[4096,1024]{1,0:T(8,128)(2,1)} %w_value.1, ...), custom_call_target="tpu_custom_call" | custom-call | tf_op jit(solution)/shard_map/pallas_call | solution.py:380
  57.9 0.0 copy-done.5
  57.9 0.0 copy-start
  58.0 2.2 %copy-done = f32[1024,1024]{1,0:T(8,128)S(1)} copy-done((f32[1024,1024]{1,0:T(8,128)S(1)}, f32[1024,1024]{1,0:T(8,128)}, u32[]{:S(2)}) %copy-start) | copy-done | bytes 4194328
  60.1 0.0 copy-start.1
  60.1 1.6 %copy-done.1 = bf16[1024,1024]{1,0:T(8,128)(2,1)S(1)} copy-done((bf16[1024,1024]{1,0:T(8,128)(2,1)S(1)}, bf16[1024,1024]{1,0:T(8,128)(2,1)}, u32[]{:S(2)}) %copy-start.1) | copy-done | bytes 2097176
  61.7 0.0 copy-start.3
  61.7 1.2 copy-done.3
  63.0 0.0 copy-start.4
  63.0 1.2 copy-done.4
  64.2 32.1 %shard_map.105 = (bf16[1024,1024]{1,0:T(8,128)(2,1)S(1)}, f32[32,256,1024]{2,1,0:T(8,128)}) custom-call(f32[1024,2]{1,0:T(8,128)S(1)} %bitcast.5, f32[32,2,32]{2,1,0:T(2,128)S(1)} %bitcast.6, bf16[1024,512]{1,0:T(8,128)(2,1)S(1)} %copy-done.3, bf16[1024,512]{1,0:T(8,128)(2,1)S(1)} %copy-done.4, bf16[1024,1024]{1,0:T(8,128)(2,1)S(1)} %copy-done.1, ...), custom_call_target="tpu_custom_call" | custom-call | flops 3221225472 | bytes 67108864 | tf_op jit(solution)/shard_map/pallas_call | solution.py:184
  96.2 0.0 copy-start.2
  96.2 1.3 copy-done.2
  97.6 43.9 %shard_map.106 = bf16[1024,512]{1,0:T(8,128)(2,1)} custom-call(bf16[1024,1024]{1,0:T(8,128)(2,1)} %copy-done.2, bf16[1024,4096]{1,0:T(8,128)(2,1)} %w_out.1), custom_call_target="tpu_custom_call" | custom-call | tf_op jit(solution)/shard_map/pallas_call | solution.py:512
  141.5 2.3 %copy.21 = bf16[1024,512]{1,0:T(8,128)(2,1)} copy(bf16[1024,512]{1,0:T(8,128)(2,1)} %shard_map.106) | data formatting | bytes 2097152
  (2 shorter events, 0.0 us)
Async XLA Ops:
  2.2 55.7 %copy-start.5 = (f32[1024]{0:T(1024)S(1)}, f32[1024]{0:T(1024)}, u32[]{:S(2)}) copy-start(f32[1024]{0:T(1024)} %param.17) | copy-start | bytes 12292
  57.9 2.2 %copy-start = (f32[1024,1024]{1,0:T(8,128)S(1)}, f32[1024,1024]{1,0:T(8,128)}, u32[]{:S(2)}) copy-start(f32[1024,1024]{1,0:T(8,128)} %get-tuple-element.11.gate) | copy-start | bytes 12582916
  60.1 1.6 %copy-start.1 = (bf16[1024,1024]{1,0:T(8,128)(2,1)S(1)}, bf16[1024,1024]{1,0:T(8,128)(2,1)}, u32[]{:S(2)}) copy-start(bf16[1024,1024]{1,0:T(8,128)(2,1)} %get-tuple-element.10.v) | copy-start | bytes 6291460
  61.7 1.2 copy-start.3
  63.0 1.2 copy-start.4
  96.2 1.3 copy-start.2
where the time goes:
time: 145 us; the launch traced here: 144 us
  Pallas kernels  132 us (91%)
  local copies, waits for them, and re-layouts  11 us (8%)
    pallas_call x1, Pallas kernels, gather_project(): pl.pallas_call(functools.partial(project_kernel, chunks), in_specs=[anywh...  55.7 us
    pallas_call x1, Pallas kernels, project_out(): pl.pallas_call(functools.partial(output_kernel, chunks), in_specs=[anywhe...  43.9 us
    pallas_call x1, Pallas kernels, retention(): pl.pallas_call(functools.partial(retention_step, per_step, groups), grid=...  32.1 us
    unnamed x13, local copies, waits for them, and re-layouts  9.83 us

commit v1 on v0

v1 whole, which is shorter than its diff:
```python
import functools

import jax
import jax.numpy as jnp
from jax import lax
from jax.experimental import pallas as pl
from jax.experimental.pallas import tpu as pltpu
from jax.sharding import PartitionSpec as P

HEAD = 256
VHEAD = 512
NEW = 32


EPS = 0.1


def partner(shard, axis, bit):
    return lax.ppermute(shard, axis, [(i, i ^ 1 << bit) for i in range(lax.axis_size(axis))])


def split_heads(tokens, decay, state, w_query, w_key, w_value, w_gate, w_out, norm_gain):
    highest = lax.Precision.HIGHEST
    tok_rows = tokens.shape[0]
    qk_columns = w_query.shape[1]
    v_columns = w_value.shape[1]
    head_span = max(1, HEAD // qk_columns)
    groups = max(1, qk_columns // HEAD)
    qk_width = qk_columns // groups
    v_width = v_columns // groups
    sequences = tok_rows // NEW
    bit_count = head_span.bit_length() - 1
    device_index = lax.axis_index("mp")
    first_head = device_index * qk_columns // HEAD
    qk_zeros = jnp.zeros((tok_rows, qk_columns), jnp.float32)
    v_zeros = jnp.zeros((tok_rows, v_columns), jnp.float32)
    carried = (qk_zeros, qk_zeros, v_zeros, v_zeros)
    segment = lax.all_gather(tokens, "mp", axis=1, tiled=True)
    updated = []
    for running, weight in zip(carried, (w_query, w_key, w_value, w_gate)):
        updated.append(jnp.dot(segment, weight, preferred_element_type=jnp.float32))
    query, key_proj, value_proj, gate_proj = tuple(updated)
    query = (query * HEAD ** (-0.5)).astype(jnp.bfloat16).reshape(tok_rows, groups, qk_width)
    key_proj = key_proj.astype(jnp.bfloat16).reshape(tok_rows, groups, qk_width)
    value_proj = value_proj.astype(jnp.bfloat16)
    for bit_number in range(bit_count):
        other_query, other_key = partner((query, key_proj), "mp", bit_number)
        upper_half = device_index >> bit_number & 1 == 1
        query = jnp.where(
            upper_half,
            jnp.concatenate([other_query, query], 2),
            jnp.concatenate([query, other_query], 2),
        )
        key_proj = jnp.where(
            upper_half,
            jnp.concatenate([other_key, key_proj], 2),
            jnp.concatenate([key_proj, other_key], 2),
        )
    query_block = query.reshape(sequences, NEW, groups, HEAD)
    key_block = key_proj.reshape(sequences, NEW, groups, HEAD)
    value_block = value_proj.reshape(sequences, NEW, groups, v_width)
    decay_rates = lax.dynamic_slice_in_dim(decay, first_head, groups, 1).reshape(
        sequences, NEW, groups
    )
    log_cumul = jnp.cumsum(jnp.log(decay_rates), axis=1)
    old_state = state.reshape(sequences, HEAD, groups, v_width)
    from_state = jnp.einsum(
        "bngk,bkgv->bngv", query_block.astype(jnp.float32), old_state, precision=highest
    )
    scores = jnp.einsum(
        "bngk,bmgk->bgnm", query_block, key_block, preferred_element_type=jnp.float32
    )
    along = jnp.transpose(log_cumul, (0, 2, 1))
    log_gap = along[:, :, :, None] - along[:, :, None, :]
    causal = jnp.arange(NEW)[:, None] >= jnp.arange(NEW)[None, :]
    factor = jnp.where(causal, jnp.exp(jnp.where(causal, log_gap, 0.0)), 0.0)
    weights = (scores * factor).astype(jnp.bfloat16)
    in_block = jnp.einsum(
        "bgnm,bmgv->bngv", weights, value_block, preferred_element_type=jnp.float32
    )
    retained = jnp.exp(log_cumul)[..., None] * from_state + in_block
    final_log = log_cumul[:, -1, :]
    carry_scale = jnp.exp(final_log[:, None, :] - log_cumul)
    decayed_keys = key_block.astype(jnp.float32) * carry_scale[..., None]
    fresh = jnp.einsum(
        "bngk,bngv->bkgv", decayed_keys, value_block.astype(jnp.float32), precision=highest
    )
    new_state = jnp.exp(final_log)[:, None, :, None] * old_state + fresh
    new_state = new_state.reshape(sequences, HEAD, v_columns)
    retained = retained.reshape(tok_rows, groups, v_width)
    running = jnp.sum(retained, axis=-1)
    squares = jnp.sum(retained * retained, axis=-1)
    for bit_number in range(bit_count):
        other_sum, other_square = partner((running, squares), "mp", bit_number)
        running = running + other_sum
        squares = squares + other_square
    centre = running / VHEAD
    variance = squares / VHEAD - centre * centre
    deviation = retained - centre[..., None]
    normed = deviation * lax.rsqrt(variance + EPS)[..., None]
    gated_out = (normed.reshape(tok_rows, v_columns) * norm_gain * jax.nn.silu(gate_proj)).astype(
        jnp.bfloat16
    )
    partial_terms = jnp.dot(gated_out, w_out, preferred_element_type=jnp.float32)
    layer_out = lax.psum_scatter(partial_terms, "mp", scatter_dimension=1, tiled=True).astype(
        jnp.bfloat16
    )
    return (layer_out, new_state)


CHUNKS = 8
EXCHANGED = 5
TILE = 512
PER_STEP = 2


def partners(device):
    core = device % 2
    across_x = device + 2 - 4 * ((device // 2) % 2)
    across_y = device + 4 - 8 * (device // 4)
    near = across_x + core * (across_y - across_x)
    far = across_y + core * (across_x - across_y)
    return near, far, across_x + across_y - device, device + 1 - 2 * core


def meet(devices):
    barrier = pltpu.get_barrier_semaphore()
    for device in devices:
        pl.semaphore_signal(
            barrier, inc=1, device_id={"mp": device}, device_id_type=pl.DeviceIdType.MESH
        )
    pl.semaphore_wait(barrier, len(devices))


def remote(source, target, send, recv, device):
    return pltpu.make_async_remote_copy(
        src_ref=source,
        dst_ref=target,
        send_sem=send,
        recv_sem=recv,
        device_id={"mp": device},
        device_id_type=pl.DeviceIdType.MESH,
    )


def fused_kernel(
    chunks,
    reduced,
    groups,
    tokens,
    w_query,
    w_key,
    w_value,
    w_gate,
    w_out,
    state,
    c_col,
    c_row,
    gain,
    key_out,
    value_out,
    layer_out,
    own_out,
    near_out,
    far_out,
    diag_out,
    gathered,
    wq,
    wk,
    wv,
    wg,
    wo,
    q_held,
    k_held,
    v_held,
    g_held,
    s_held,
    gated,
    to_sibling,
    from_sibling,
    outgoing,
    incoming,
    total,
    pending,
    finished,
    load_sem,
    state_sem,
    kv_sem,
    out_sem,
    send,
    recv,
    sum_send,
    sum_recv,
):
    me = lax.axis_index("mp")
    near, far, diagonal, sibling = partners(me)
    sib_near, sib_far, sib_diagonal, _ = partners(sibling)
    mine = (me, near, far, diagonal)
    theirs = (sibling, sib_near, sib_far, sib_diagonal)
    rows, width = tokens.shape
    size = rows // chunks
    sequences = size // NEW
    vw = w_value.shape[1] // groups

    def at(r):
        return pl.ds(pl.multiple_of(r * size, size), size)

    def span(device):
        return pl.ds(pl.multiple_of(device * width, width), width)

    def copy(lane, source, target, r):
        there = gathered.at[at(r), span(source)]
        return remote(there, there, send.at[lane, r], recv.at[lane, r], target)

    def swap(j, r):
        return remote(
            to_sibling.at[lax.rem(r, 2), j],
            from_sibling.at[j, at(r), :],
            sum_send.at[j, r],
            sum_recv.at[j, r],
            sibling,
        )

    def hop(lane, r):
        return remote(
            outgoing.at[lane, at(r), :],
            incoming.at[lane, at(r), :],
            sum_send.at[4 + lane, r],
            sum_recv.at[4 + lane, r],
            near if lane == 0 else far,
        )

    own = pltpu.make_async_copy(tokens, gathered.at[:, span(me)], load_sem.at[0])
    own.start()
    loads = [
        pltpu.make_async_copy(source, held, load_sem.at[1 + n])
        for n, (source, held) in enumerate(
            ((w_query, wq), (w_key, wk), (w_value, wv), (w_gate, wg), (w_out, wo))
        )
    ]
    for load in loads:
        load.start()

    def load_state(r):
        first = pl.multiple_of(r * sequences, sequences)
        return pltpu.make_async_copy(
            state.at[pl.ds(first, sequences)], s_held, state_sem.at[0]
        )

    def store_key(r):
        return pltpu.make_async_copy(
            k_held.at[lax.rem(r, 2)], key_out.at[at(r), :], kv_sem.at[0, r]
        )

    def store_value(r):
        return pltpu.make_async_copy(
            v_held.at[lax.rem(r, 2)], value_out.at[at(r), :], kv_sem.at[1, r]
        )

    def store_layer(r):
        return pltpu.make_async_copy(
            finished.at[at(r), :], layer_out.at[at(r), :], out_sem.at[0, r]
        )

    def store_shares(r):
        there = at(r - reduced)
        return [pltpu.make_async_copy(total.at[at(r), :], own_out.at[there, :], out_sem.at[0, r])] + [
            pltpu.make_async_copy(
                outgoing.at[lane, at(r), :], target.at[there, :], out_sem.at[1 + lane, r]
            )
            for lane, target in enumerate((near_out, far_out, diag_out))
        ]

    meet((near, far, sibling))
    own.wait()

    def pass_near(r):
        copy(0, near, near, r).wait_recv()
        copy(2, near, far, r).start()
        copy(4, near, sibling, r).start()

    def pass_far(r):
        copy(1, far, far, r).wait_recv()
        copy(5, far, sibling, r).start()

    def pass_diagonal(r):
        copy(2, diagonal, far, r).wait_recv()
        copy(6, diagonal, sibling, r).start()

    copy(0, me, near, 0).start()
    copy(1, me, far, 0).start()
    copy(3, me, sibling, 0).start()
    copy(0, me, near, 1).start()
    pass_near(0)
    copy(1, me, far, 1).start()
    copy(3, me, sibling, 1).start()
    copy(0, me, near, 2).start()
    pass_far(0)
    pass_diagonal(0)
    pass_near(1)
    copy(1, me, far, 2).start()
    copy(3, me, sibling, 2).start()
    pass_far(1)

    place = lax.broadcasted_iota(jnp.int32, (size, size), 0)
    other = lax.broadcasted_iota(jnp.int32, (size, size), 1)
    causal = (place >= other) & (place // NEW == other // NEW)

    def project(r, weight, col, stop):
        return jnp.dot(
            gathered[at(r), :], weight[:, col:stop], preferred_element_type=jnp.float32
        )

    def share(dest):
        return jnp.dot(gated[...], wo[:, span(dest)], preferred_element_type=jnp.float32)

    def relay(r):
        hop(2, r).wait_recv()
        part = pending[lax.rem(r, 2)] + incoming[2, at(r), :].astype(jnp.float32)
        outgoing[0, at(r), :] = part.astype(jnp.bfloat16)
        hop(0, r).start()

    def finish(r):
        hop(1, r).wait_recv()
        hop(0, r).wait_recv()
        finished[at(r), :] = (
            total[at(r), :]
            + incoming[0, at(r), :].astype(jnp.float32)
            + incoming[1, at(r), :].astype(jnp.float32)
        ).astype(jnp.bfloat16)
        store_layer(r).start()

    def step(r, carry):
        slot = lax.rem(r, 2)
        load_state(r).start()
        for lane, source in ((3, sibling), (4, sib_near), (5, sib_far), (6, sib_diagonal)):
            copy(lane, source, sibling, r).wait_recv()

        @pl.when(r == 0)
        def _():
            loads[0].wait()
            loads[1].wait()

        @pl.when(r >= 2)
        def _():
            store_key(r - 2).wait()
            store_value(r - 2).wait()

        for col in range(0, wq.shape[1], TILE):
            stop = min(col + TILE, wq.shape[1])
            q_held[:, col:stop] = (project(r, wq, col, stop) * HEAD ** (-0.5)).astype(jnp.bfloat16)
            k_held[slot, :, col:stop] = project(r, wk, col, stop).astype(jnp.bfloat16)
        store_key(r).start()

        @pl.when(r + 1 < chunks)
        def _():
            pass_diagonal(r + 1)

        @pl.when((r >= 1) & (r - 1 < reduced))
        def _():
            relay(r - 1)

        @pl.when(r == 0)
        def _():
            loads[2].wait()
            loads[3].wait()

        for col in range(0, wv.shape[1], TILE):
            stop = min(col + TILE, wv.shape[1])
            v_held[slot, :, col:stop] = project(r, wv, col, stop).astype(jnp.bfloat16)
        store_value(r).start()

        @pl.when(r + 2 < chunks)
        def _():
            pass_near(r + 2)
            pass_far(r + 2)

        @pl.when(r + 3 < chunks)
        def _():
            copy(0, me, near, r + 3).start()
            copy(1, me, far, r + 3).start()
            copy(3, me, sibling, r + 3).start()

        for col in range(0, wg.shape[1], TILE):
            stop = min(col + TILE, wg.shape[1])
            gates = project(r, wg, col, stop)
            g_held[:, col:stop] = gain[:, col:stop] * (gates / (1.0 + jnp.exp(-gates)))

        load_state(r).wait()
        for g in range(groups):
            vs = slice(g * vw, (g + 1) * vw)
            ks = slice(g * HEAD, (g + 1) * HEAD)
            query, key, value = q_held[:, ks], k_held[slot, :, ks], v_held[slot, :, vs]
            col = c_col[at(r), g : g + 1]
            row = c_row[r, g : g + 1, :]
            scores = lax.dot_general(
                query, key, (((1,), (1,)), ((), ())), preferred_element_type=jnp.float32
            )
            factor = jnp.where(causal, jnp.exp(jnp.where(causal, col - row, 0.0)), 0.0)
            weights = (scores * factor).astype(jnp.bfloat16)
            from_state = jnp.concatenate(
                [
                    jnp.dot(
                        query[s * NEW : (s + 1) * NEW],
                        s_held[s, :, vs].astype(jnp.bfloat16),
                        preferred_element_type=jnp.float32,
                    )
                    for s in range(sequences)
                ],
                axis=0,
            )
            in_block = jnp.dot(weights, value, preferred_element_type=jnp.float32)
            retained = jnp.exp(col) * from_state + in_block
            centre = jnp.mean(retained, axis=1, keepdims=True)
            deviation = retained - centre
            variance = jnp.mean(deviation * deviation, axis=1, keepdims=True)
            normed = deviation * lax.rsqrt(variance + EPS)
            gated[:, vs] = (normed * g_held[:, vs]).astype(jnp.bfloat16)

        @pl.when(r == 0)
        def _():
            loads[4].wait()

        for j in (3, 2, 1, 0):

            @pl.when(r >= 2)
            def _():
                swap(j, r - 2).wait_send()

            to_sibling[slot, j] = share(theirs[j]).astype(jnp.bfloat16)
            swap(j, r).start()

        @pl.when((r >= 2) & (r - 2 < reduced))
        def _():
            finish(r - 2)

        for j in (3, 2, 1, 0):
            part = share(mine[j])
            swap(j, r).wait_recv()
            part = part + from_sibling[j, at(r), :].astype(jnp.float32)
            if j >= 2:
                outgoing[j - 1, at(r), :] = part.astype(jnp.bfloat16)

                @pl.when(r < reduced)
                def _():
                    hop(j - 1, r).start()
            elif j == 1:
                pending[slot] = part

                @pl.when(r >= reduced)
                def _():
                    outgoing[0, at(r), :] = part.astype(jnp.bfloat16)
            else:
                total[at(r), :] = part

        @pl.when(r >= reduced)
        def _():
            for store in store_shares(r):
                store.start()

        return carry

    lax.fori_loop(0, chunks, step, 0)
    if reduced == chunks:
        relay(reduced - 1)
    for r in (chunks - 2, chunks - 1):
        if r < reduced:
            finish(r)

    def drain(r, carry):
        for lane, (source, target) in enumerate(
            (
                (me, near),
                (me, far),
                (near, far),
                (me, sibling),
                (near, sibling),
                (far, sibling),
                (diagonal, sibling),
            )
        ):
            copy(lane, source, target, r).wait_send()

        @pl.when(r >= chunks - 2)
        def _():
            store_key(r).wait()
            store_value(r).wait()
            for j in range(4):
                swap(j, r).wait_send()

        @pl.when(r < reduced)
        def _():
            for lane in range(3):
                hop(lane, r).wait_send()
            store_layer(r).wait()

        @pl.when(r >= reduced)
        def _():
            for store in store_shares(r):
                store.wait()

        return carry

    lax.fori_loop(0, chunks, drain, 0)


def fused(tokens, w_query, w_key, w_value, w_gate, w_out, state, c_col, c_row, gain):
    rows, width = tokens.shape
    depth, qk = w_query.shape
    vc = w_value.shape[1]
    chunks, reduced = CHUNKS, EXCHANGED
    size = rows // chunks
    groups = c_col.shape[1]
    kept = reduced * size
    rest = rows - kept
    anywhere = pl.BlockSpec(memory_space=pl.ANY)
    vmem = pl.BlockSpec(memory_space=pltpu.VMEM)
    narrow = jnp.bfloat16
    wide = jnp.float32
    shapes = [
        ((rows, qk), narrow),
        ((rows, vc), narrow),
        ((kept, width), narrow),
        ((rest, width), wide),
        ((rest, width), narrow),
        ((rest, width), narrow),
        ((rest, width), narrow),
    ]
    return pl.pallas_call(
        functools.partial(fused_kernel, chunks, reduced, groups),
        in_specs=[anywhere] * 7 + [vmem] * 3,
        out_specs=[anywhere] * len(shapes),
        out_shape=[jax.ShapeDtypeStruct(*shape) for shape in shapes],
        scratch_shapes=[
            pltpu.VMEM((rows, depth), narrow),
            pltpu.VMEM((depth, qk), narrow),
            pltpu.VMEM((depth, qk), narrow),
            pltpu.VMEM((depth, vc), narrow),
            pltpu.VMEM((depth, vc), narrow),
            pltpu.VMEM(w_out.shape, narrow),
            pltpu.VMEM((size, qk), narrow),
            pltpu.VMEM((2, size, qk), narrow),
            pltpu.VMEM((2, size, vc), narrow),
            pltpu.VMEM((size, vc), wide),
            pltpu.VMEM((size // NEW,) + state.shape[1:], wide),
            pltpu.VMEM((size, vc), narrow),
            pltpu.VMEM((2, 4, size, width), narrow),
            pltpu.VMEM((4, rows, width), narrow),
            pltpu.VMEM((3, rows, width), narrow),
            pltpu.VMEM((3, kept, width), narrow),
            pltpu.VMEM((rows, width), wide),
            pltpu.VMEM((2, size, width), wide),
            pltpu.VMEM((kept, width), narrow),
            pltpu.SemaphoreType.DMA((6,)),
            pltpu.SemaphoreType.DMA((1,)),
            pltpu.SemaphoreType.DMA((2, chunks)),
            pltpu.SemaphoreType.DMA((4, chunks)),
            pltpu.SemaphoreType.DMA((7, chunks)),
            pltpu.SemaphoreType.DMA((7, chunks)),
            pltpu.SemaphoreType.DMA((7, chunks)),
            pltpu.SemaphoreType.DMA((7, chunks)),
        ],
        compiler_params=pltpu.CompilerParams(
            collective_id=0, has_side_effects=True, vmem_limit_bytes=67043328
        ),
        cost_estimate=pl.CostEstimate(
            flops=2 * rows * depth * (2 * qk + 3 * vc),
            bytes_accessed=4 * state.size,
            transcendentals=rows * vc,
        ),
    )(tokens, w_query, w_key, w_value, w_gate, w_out, state, c_col, c_row, gain)


def update_step(per_step, groups, c_col, k, v, state, new_state):
    vw = v.shape[1] // groups
    for s in range(per_step):
        at = slice(s * NEW, (s + 1) * NEW)
        for g in range(groups):
            vs = slice(g * vw, (g + 1) * vw)
            col = c_col[at, g : g + 1]
            last = col[NEW - 1 : NEW, :]
            key = k[at, g * HEAD : (g + 1) * HEAD].astype(jnp.float32)
            scaled = (key * jnp.exp(last - col)).astype(jnp.bfloat16)
            fresh = lax.dot_general(
                scaled, v[at, vs], (((0,), (0,)), ((), ())), preferred_element_type=jnp.float32
            )
            new_state[s, :, vs] = jnp.exp(last) * state[s, :, vs] + fresh


def update_state(c_col, k, v, state):
    rows, groups = c_col.shape
    sequences = rows // NEW
    per_step = PER_STEP if sequences % PER_STEP == 0 else 1
    by_row = lambda width: pl.BlockSpec((per_step * NEW, width), lambda i: (i, 0))
    state_spec = pl.BlockSpec((per_step,) + state.shape[1:], lambda i: (i, 0, 0))
    return pl.pallas_call(
        functools.partial(update_step, per_step, groups),
        grid=(sequences // per_step,),
        in_specs=[by_row(groups), by_row(k.shape[1]), by_row(v.shape[1]), state_spec],
        out_specs=state_spec,
        out_shape=jax.ShapeDtypeStruct(state.shape, jnp.float32),
        compiler_params=pltpu.CompilerParams(
            dimension_semantics=("arbitrary",), vmem_limit_bytes=60 << 20
        ),
        cost_estimate=pl.CostEstimate(
            flops=2 * rows * HEAD * v.shape[1],
            bytes_accessed=8 * state.size,
            transcendentals=rows,
        ),
    )(c_col, k, v, state)


def whole_heads(tokens, decay, state, w_query, w_key, w_value, w_gate, w_out, norm_gain):
    tok_rows = tokens.shape[0]
    groups = w_query.shape[1] // HEAD
    sequences = tok_rows // NEW
    first_head = lax.axis_index("mp") * groups
    logs = jnp.log(lax.dynamic_slice_in_dim(decay, first_head, groups, 1))
    logs = logs.reshape(sequences, NEW, groups)
    causal = jnp.arange(NEW)[:, None] >= jnp.arange(NEW)[None, :]
    cumul = jnp.sum(jnp.where(causal[None, :, :, None], logs[:, None], 0.0), axis=2)
    c_col = cumul.reshape(tok_rows, groups)
    c_row = jnp.transpose(cumul.reshape(CHUNKS, tok_rows // CHUNKS, groups), (0, 2, 1))
    key_proj, value_proj, reduced, own, *shares = fused(
        tokens,
        w_query,
        w_key,
        w_value,
        w_gate,
        w_out,
        state,
        c_col,
        c_row,
        norm_gain.reshape(1, -1),
    )
    devices = range(lax.axis_size("mp"))
    for n, share in enumerate(shares):
        pairs = [(device, partners(device)[n]) for device in devices]
        own = own + lax.ppermute(share, "mp", pairs).astype(jnp.float32)
    layer_out = jnp.concatenate([reduced, own.astype(jnp.bfloat16)])
    return (layer_out, update_state(c_col, key_proj, value_proj, state))


def per_device(tokens, decay, state, w_query, *rest):
    whole = w_query.shape[1] % HEAD == 0 and lax.axis_size("mp") == 8
    path = whole_heads if whole else split_heads
    return path(tokens, decay, state, w_query, *rest)


def solution(mesh):
    placed = (
        P("dp", "mp"),
        P("dp", None),
        P("dp", None, "mp"),
        P(None, "mp"),
        P(None, "mp"),
        P(None, "mp"),
        P(None, "mp"),
        P("mp", None),
        P("mp"),
    )
    return jax.shard_map(
        per_device,
        mesh=mesh,
        in_specs=placed,
        out_specs=(P("dp", "mp"), P("dp", None, "mp")),
        check_vma=False,
    )
```

time: 145 us -> 129 us (0.89)
  Pallas kernels: 132 us -> 120 us
  local copies, waits for them, and re-layouts: 11 us -> 2.64 us
  starting transfers between devices: 0 us -> 3.55 us
    pallas_call x3 -> x2, Pallas kernels: 132 us -> 120 us  [the longest x1 88.5 us: fused(): pl.pallas_call(functools.partial(fused_kernel, chunks, reduced, groups),...]
    unnamed x13 -> x4, local copies, waits for them, and re-layouts: 9.83 us -> 0.01 us
    ppermute x0 -> x3, starting transfers between devices: none -> 3.55 us  [whole_heads(): own = own + lax.ppermute(share, 'mp', pairs).astype(jnp.float32)]
  transfers between devices with their start and end apart: 0 -> 3, of which waited for: 0 -> 0; matrix products, arithmetic and copies ran while one was open for 0% -> 0% of each run, Pallas kernels for 0% -> 24%
where the time goes in v1:
time: 129 us; the launch traced here: 128 us
  Pallas kernels  120 us (93%)
  starting transfers between devices  3.55 us (3%)
  local copies, waits for them, and re-layouts  2.64 us (2%)
  other arithmetic  1.65 us (1%)
    pallas_call x1, Pallas kernels, fused(): pl.pallas_call(functools.partial(fused_kernel, chunks, reduced, groups),...  88.5 us
    pallas_call x1, Pallas kernels, update_state(): pl.pallas_call(functools.partial(update_step, per_step, groups), grid=(se...  31.2 us
    ppermute x3, starting transfers between devices, whole_heads(): own = own + lax.ppermute(share, 'mp', pairs).astype(jnp.float32)  3.55 us
  transfers between devices with their start and end apart: 3, of which 0 were waited for; matrix products, arithmetic and copies ran while one was open for 0% of the time, Pallas kernels for 24%

profile of v1, /device:TPU:0, one launch (start us, length us, event | category | flops | bytes accessed | tf_op | source)
XLA Modules:
  0.0 128.3 jit_solution(10446727596659522924)
XLA Ops:
  0.7 0.8 dynamic-slice_log_fusion
  1.4 0.1 broadcast_in_dim.26
  1.6 0.4 select_reduce_fusion
  2.0 1.1 copy.16
  3.0 0.1 reshape.28
  3.1 0.6 copy.20
  3.7 88.5 %shard_map.104 = (bf16[1024,512]{1,0:T(8,128)(2,1)}, bf16[1024,1024]{1,0:T(8,128)(2,1)}, bf16[640,512]{1,0:T(8,128)(2,1)}, f32[384,512]{1,0:T(8,128)}, bf16[384,...) custom-call(bf16[1024,512]{1,0:T(8,128)(2,1)} %tokens.1, bf16[4096,512]{1,0:T(8,128)(2,1)} %w_query.1, ...), custom_call_target="tpu_custom_call" | custom-call | flops 34359738368 | bytes 33554432 | tf_op jit(solution)/shard_map/pallas_call | solution.py:529
  92.3 1.2 collective-permute-start
  93.4 0.9 collective-permute-start.1
  94.3 1.5 %collective-permute-start.2 = (bf16[384,512]{1,0:T(8,128)(2,1)}, bf16[384,512]{1,0:T(8,128)(2,1)S(1)}, u32[]{:S(2)}, u32[]{:S(2)}) collective-permute-start(bf16[384,512]{1,0:T(8,128)(2,1)} %get-tuple-element.13), channel_id=1, source_target_pairs={{0,6},{1,7},{2,4},{3,5},{4,2},{5,3},{6,0},{7,1},{8,14},{9,15},{10,... | collective-permute-start | bytes 1179656 | tf_op jit(solution)/shard_map/ppermute | solution.py:639
  95.8 0.0 copy-start
  95.8 0.0 copy-start.1
  95.8 31.2 %shard_map.105 = f32[32,256,1024]{2,1,0:T(8,128)} custom-call(f32[1024,2]{1,0:T(8,128)} %bitcast.10, bf16[1024,512]{1,0:T(8,128)(2,1)} %get-tuple-element.14.k, bf16[1024,1024]{1,0:T(8,128)(2,1)} %get-tuple-element.15.v, f32[32,256,1024]{2,1,0:T(8,128)} %state.3), custom_call_target="tpu_custom_call" | custom-call | flops 536870912 | bytes 67108864 | tf_op jit(solution)/shard_map/pallas_call | solution.py:596
  127.0 0.0 collective-permute-done
  127.0 0.0 collective-permute-done.1
  127.0 0.0 collective-permute-done.2
  127.0 0.0 copy-done
  127.1 0.2 add_convert_fusion
  127.3 0.0 copy-done.1
  127.3 1.0 pad_maximum_fusion
  (3 shorter events, 0.0 us)
Async XLA Ops:
  92.3 34.8 %collective-permute-start = (bf16[384,512]{1,0:T(8,128)(2,1)}, bf16[384,512]{1,0:T(8,128)(2,1)S(1)}, u32[]{:S(2)}, u32[]{:S(2)}) collective-permute-start(bf16[384,512]{1,0:T(8,128)(2,1)} %get-tuple-element.11), channel_id=1, source_target_pairs={{0,2},{1,5},{2,0},{3,7},{4,6},{5,1},{6,4},{7,3},{8,10},{9,13},{10,... | collective-permute-start | bytes 1179656 | tf_op jit(solution)/shard_map/ppermute | solution.py:639
  93.4 33.6 %collective-permute-start.1 = (bf16[384,512]{1,0:T(8,128)(2,1)}, bf16[384,512]{1,0:T(8,128)(2,1)S(1)}, u32[]{:S(2)}, u32[]{:S(2)}) collective-permute-start(bf16[384,512]{1,0:T(8,128)(2,1)} %get-tuple-element.12), channel_id=1, source_target_pairs={{0,4},{1,3},{2,6},{3,1},{4,0},{5,7},{6,2},{7,5},{8,12},{9,11},{10,... | collective-permute-start | bytes 1179656 | tf_op jit(solution)/shard_map/ppermute | solution.py:639
  94.3 32.7 %collective-permute-start.2 = (bf16[384,512]{1,0:T(8,128)(2,1)}, bf16[384,512]{1,0:T(8,128)(2,1)S(1)}, u32[]{:S(2)}, u32[]{:S(2)}) collective-permute-start(bf16[384,512]{1,0:T(8,128)(2,1)} %get-tuple-element.13), channel_id=1, source_target_pairs={{0,6},{1,7},{2,4},{3,5},{4,2},{5,3},{6,0},{7,1},{8,14},{9,15},{10,... | collective-permute-start | bytes 1179656 | tf_op jit(solution)/shard_map/ppermute | solution.py:639
  95.8 31.2 %copy-start = (f32[384,512]{1,0:T(8,128)S(1)}, f32[384,512]{1,0:T(8,128)}, u32[]{:S(2)}) copy-start(f32[384,512]{1,0:T(8,128)} %get-tuple-element.10) | copy-start | bytes 2359300
  95.8 31.5 %copy-start.1 = (bf16[640,512]{1,0:T(8,128)(2,1)S(1)}, bf16[640,512]{1,0:T(8,128)(2,1)}, u32[]{:S(2)}) copy-start(bf16[640,512]{1,0:T(8,128)(2,1)} %get-tuple-element.9) | copy-start | bytes 1966084

commit v2 on v1

--- a/solution.py
+++ b/solution.py
@@ -109,9 +109,9 @@
 
 
 CHUNKS = 8
-EXCHANGED = 5
+EXCHANGED = 2
 TILE = 512
-PER_STEP = 2
+DEPTH = 8
 
 
 def partners(device):
@@ -154,16 +154,15 @@
     w_gate,
     w_out,
     state,
-    c_col,
-    c_row,
+    decay,
     gain,
     key_out,
     value_out,
+    decay_out,
     layer_out,
     own_out,
     near_out,
     far_out,
-    diag_out,
     gathered,
     wq,
     wk,
@@ -181,8 +180,11 @@
     outgoing,
     incoming,
     total,
+    parts,
     pending,
     finished,
+    cumul,
+    cumul_row,
     load_sem,
     state_sem,
     kv_sem,
@@ -268,7 +270,7 @@
             pltpu.make_async_copy(
                 outgoing.at[lane, at(r), :], target.at[there, :], out_sem.at[1 + lane, r]
             )
-            for lane, target in enumerate((near_out, far_out, diag_out))
+            for lane, target in enumerate((near_out, far_out))
         ]
 
     meet((near, far, sibling))
@@ -287,20 +289,45 @@
         copy(2, diagonal, far, r).wait_recv()
         copy(6, diagonal, sibling, r).start()
 
+    def give_far(r):
+        copy(1, me, far, r).start()
+        copy(3, me, sibling, r).start()
+
     copy(0, me, near, 0).start()
-    copy(1, me, far, 0).start()
-    copy(3, me, sibling, 0).start()
+    give_far(0)
     copy(0, me, near, 1).start()
+
+    head = lax.broadcasted_iota(jnp.int32, (decay.shape[0], size), 0)
+    token = lax.broadcasted_iota(jnp.int32, (8, size), 1) % NEW
+    place = lax.broadcasted_iota(jnp.int32, (8, size), 0)
+
+    def accumulate(r, carry):
+        logs = jnp.log(decay[:, at(r)])
+        sums = jnp.zeros((8, size), jnp.float32)
+        for g in range(groups):
+            chosen = jnp.where(head == me * groups + g, logs, 0.0)
+            sums = jnp.where(place == g, jnp.sum(chosen, axis=0, keepdims=True), sums)
+        shift = 1
+        while shift < NEW:
+            sums = sums + jnp.where(token >= shift, pltpu.roll(sums, shift, 1), 0.0)
+            shift *= 2
+        cumul_row[r] = sums
+        cumul[at(r), :] = jnp.transpose(sums)
+        return carry
+
     pass_near(0)
-    copy(1, me, far, 1).start()
-    copy(3, me, sibling, 1).start()
+    give_far(1)
     copy(0, me, near, 2).start()
     pass_far(0)
+    lax.fori_loop(0, chunks, accumulate, 0)
+    decay_copy = pltpu.make_async_copy(cumul, decay_out, load_sem.at[6])
+    decay_copy.start()
     pass_diagonal(0)
     pass_near(1)
-    copy(1, me, far, 2).start()
-    copy(3, me, sibling, 2).start()
+    give_far(2)
+    copy(0, me, near, 3).start()
     pass_far(1)
+    give_far(3)
 
     place = lax.broadcasted_iota(jnp.int32, (size, size), 0)
     other = lax.broadcasted_iota(jnp.int32, (size, size), 1)
@@ -313,12 +340,38 @@
 
     def share(dest):
         return jnp.dot(gated[...], wo[:, span(dest)], preferred_element_type=jnp.float32)
+
+    def combine(r):
+        slot = lax.rem(r, 2)
+        for j in (3, 2, 1, 0):
+            swap(j, r).wait_recv()
+        for j in (3, 2, 1, 0):
+            part = parts[slot, j] + from_sibling[j, at(r), :].astype(jnp.float32)
+            if j >= 2:
+                outgoing[j - 1, at(r), :] = part.astype(jnp.bfloat16)
+            elif j == 1:
+                pending[slot] = part
+            else:
+                total[at(r), :] = part
+        hop(2, r).start()
+
+        @pl.when(r < reduced)
+        def _():
+            hop(1, r).start()
 
     def relay(r):
         hop(2, r).wait_recv()
         part = pending[lax.rem(r, 2)] + incoming[2, at(r), :].astype(jnp.float32)
         outgoing[0, at(r), :] = part.astype(jnp.bfloat16)
-        hop(0, r).start()
+
+        @pl.when(r < reduced)
+        def _():
+            hop(0, r).start()
+
+        @pl.when(r >= reduced)
+        def _():
+            for store in store_shares(r):
+                store.start()
 
     def finish(r):
         hop(1, r).wait_recv()
@@ -333,66 +386,67 @@
     def step(r, carry):
         slot = lax.rem(r, 2)
         load_state(r).start()
+
+        @pl.when(r + 4 < chunks)
+        def _():
+            copy(0, me, near, r + 4).start()
+            give_far(r + 4)
+
         for lane, source in ((3, sibling), (4, sib_near), (5, sib_far), (6, sib_diagonal)):
             copy(lane, source, sibling, r).wait_recv()
 
         @pl.when(r == 0)
         def _():
-            loads[0].wait()
-            loads[1].wait()
+            for load in loads:
+                load.wait()
 
         @pl.when(r >= 2)
         def _():
             store_key(r - 2).wait()
             store_value(r - 2).wait()
+            for j in range(4):
+                swap(j, r - 2).wait_send()
 
         for col in range(0, wq.shape[1], TILE):
             stop = min(col + TILE, wq.shape[1])
             q_held[:, col:stop] = (project(r, wq, col, stop) * HEAD ** (-0.5)).astype(jnp.bfloat16)
             k_held[slot, :, col:stop] = project(r, wk, col, stop).astype(jnp.bfloat16)
-        store_key(r).start()
-
-        @pl.when(r + 1 < chunks)
-        def _():
-            pass_diagonal(r + 1)
-
-        @pl.when((r >= 1) & (r - 1 < reduced))
-        def _():
-            relay(r - 1)
-
-        @pl.when(r == 0)
-        def _():
-            loads[2].wait()
-            loads[3].wait()
-
         for col in range(0, wv.shape[1], TILE):
             stop = min(col + TILE, wv.shape[1])
             v_held[slot, :, col:stop] = project(r, wv, col, stop).astype(jnp.bfloat16)
-        store_value(r).start()
-
-        @pl.when(r + 2 < chunks)
-        def _():
-            pass_near(r + 2)
-            pass_far(r + 2)
-
-        @pl.when(r + 3 < chunks)
-        def _():
-            copy(0, me, near, r + 3).start()
-            copy(1, me, far, r + 3).start()
-            copy(3, me, sibling, r + 3).start()
-
         for col in range(0, wg.shape[1], TILE):
             stop = min(col + TILE, wg.shape[1])
             gates = project(r, wg, col, stop)
             g_held[:, col:stop] = gain[:, col:stop] * (gates / (1.0 + jnp.exp(-gates)))
+
+        store_key(r).start()
+        store_value(r).start()
+
+        @pl.when(r == 0)
+        def _():
+            pass_diagonal(1)
+            pass_near(2)
+            pass_far(2)
+
+        @pl.when(r >= 2)
+        def _():
+            relay(r - 2)
+
+        @pl.when(r >= 1)
+        def _():
+            combine(r - 1)
+
+        @pl.when((r >= 4) & (r - 4 < reduced))
+        def _():
+            finish(r - 4)
 
         load_state(r).wait()
         for g in range(groups):
             vs = slice(g * vw, (g + 1) * vw)
             ks = slice(g * HEAD, (g + 1) * HEAD)
             query, key, value = q_held[:, ks], k_held[slot, :, ks], v_held[slot, :, vs]
-            col = c_col[at(r), g : g + 1]
-            row = c_row[r, g : g + 1, :]
+            col = cumul[at(r), g : g + 1]
+            row = cumul_row[r, g : g + 1, :]
             scores = lax.dot_general(
                 query, key, (((1,), (1,)), ((), ())), preferred_element_type=jnp.float32
             )
@@ -417,55 +471,31 @@
             normed = deviation * lax.rsqrt(variance + EPS)
             gated[:, vs] = (normed * g_held[:, vs]).astype(jnp.bfloat16)
 
-        @pl.when(r == 0)
-        def _():
-            loads[4].wait()
-
         for j in (3, 2, 1, 0):
-
-            @pl.when(r >= 2)
-            def _():
-                swap(j, r - 2).wait_send()
-
             to_sibling[slot, j] = share(theirs[j]).astype(jnp.bfloat16)
+        for j in (3, 2, 1, 0):
+            parts[slot, j] = share(mine[j])
+        for j in (3, 2, 1, 0):
             swap(j, r).start()
 
-        @pl.when((r >= 2) & (r - 2 < reduced))
-        def _():
-            finish(r - 2)
-
-        for j in (3, 2, 1, 0):
-            part = share(mine[j])
-            swap(j, r).wait_recv()
-            part = part + from_sibling[j, at(r), :].astype(jnp.float32)
-            if j >= 2:
-                outgoing[j - 1, at(r), :] = part.astype(jnp.bfloat16)
-
-                @pl.when(r < reduced)
-                def _():
-                    hop(j - 1, r).start()
-            elif j == 1:
-                pending[slot] = part
-
-                @pl.when(r >= reduced)
-                def _():
-                    outgoing[0, at(r), :] = part.astype(jnp.bfloat16)
-            else:
-                total[at(r), :] = part
-
-        @pl.when(r >= reduced)
-        def _():
-            for store in store_shares(r):
-                store.start()
+        @pl.when(r + 2 < chunks)
+        def _():
+            pass_diagonal(r + 2)
+
+        @pl.when(r + 3 < chunks)
+        def _():
+            pass_near(r + 3)
+            pass_far(r + 3)
 
         return carry
 
     lax.fori_loop(0, chunks, step, 0)
-    if reduced == chunks:
-        relay(reduced - 1)
-    for r in (chunks - 2, chunks - 1):
-        if r < reduced:
-            finish(r)
+    combine(chunks - 1)
+    relay(chunks - 2)
+    relay(chunks - 1)
+    for r in range(chunks - 4, reduced):
+        finish(r)
+    decay_copy.wait()
 
     def drain(r, carry):
         for lane, (source, target) in enumerate(
@@ -488,9 +518,11 @@
             for j in range(4):
                 swap(j, r).wait_send()
 
+        hop(2, r).wait_send()
+
         @pl.when(r < reduced)
         def _():
-            for lane in range(3):
+            for lane in range(2):
                 hop(lane, r).wait_send()
             store_layer(r).wait()
 
@@ -504,13 +536,13 @@
     lax.fori_loop(0, chunks, drain, 0)
 
 
-def fused(tokens, w_query, w_key, w_value, w_gate, w_out, state, c_col, c_row, gain):
+def fused(tokens, w_query, w_key, w_value, w_gate, w_out, state, decay, gain):
     rows, width = tokens.shape
     depth, qk = w_query.shape
     vc = w_value.shape[1]
     chunks, reduced = CHUNKS, EXCHANGED
     size = rows // chunks
-    groups = c_col.shape[1]
+    groups = qk // HEAD
     kept = reduced * size
     rest = rows - kept
     anywhere = pl.BlockSpec(memory_space=pl.ANY)
@@ -520,15 +552,15 @@
     shapes = [
         ((rows, qk), narrow),
         ((rows, vc), narrow),
+        ((rows, 8), wide),
         ((kept, width), narrow),
         ((rest, width), wide),
-        ((rest, width), narrow),
         ((rest, width), narrow),
         ((rest, width), narrow),
     ]
     return pl.pallas_call(
         functools.partial(fused_kernel, chunks, reduced, groups),
-        in_specs=[anywhere] * 7 + [vmem] * 3,
+        in_specs=[anywhere] * 7 + [vmem] * 2,
         out_specs=[anywhere] * len(shapes),
         out_shape=[jax.ShapeDtypeStruct(*shape) for shape in shapes],
         scratch_shapes=[
@@ -547,11 +579,14 @@
             pltpu.VMEM((2, 4, size, width), narrow),
             pltpu.VMEM((4, rows, width), narrow),
             pltpu.VMEM((3, rows, width), narrow),
-            pltpu.VMEM((3, kept, width), narrow),
+            pltpu.VMEM((3, rows, width), narrow),
             pltpu.VMEM((rows, width), wide),
+            pltpu.VMEM((2, 4, size, width), wide),
             pltpu.VMEM((2, size, width), wide),
             pltpu.VMEM((kept, width), narrow),
-            pltpu.SemaphoreType.DMA((6,)),
+            pltpu.VMEM((rows, 8), wide),
+            pltpu.VMEM((chunks, 8, size), wide),
+            pltpu.SemaphoreType.DMA((7,)),
             pltpu.SemaphoreType.DMA((1,)),
             pltpu.SemaphoreType.DMA((2, chunks)),
             pltpu.SemaphoreType.DMA((4, chunks)),
@@ -568,40 +603,111 @@
             bytes_accessed=4 * state.size,
             transcendentals=rows * vc,
         ),
-    )(tokens, w_query, w_key, w_value, w_gate, w_out, state, c_col, c_row, gain)
-
-
-def update_step(per_step, groups, c_col, k, v, state, new_state):
+    )(tokens, w_query, w_key, w_value, w_gate, w_out, state, decay, gain)
+
+
+def update_kernel(
+    groups,
+    c_col,
+    k,
+    v,
+    state,
+    new_state,
+    c_held,
+    k_held,
+    v_held,
+    s_in,
+    s_out,
+    load_sem,
+    in_sem,
+    out_sem,
+):
     vw = v.shape[1] // groups
-    for s in range(per_step):
-        at = slice(s * NEW, (s + 1) * NEW)
+    sequences = state.shape[0]
+    depth = s_in.shape[0]
+
+    def load(s):
+        slot = lax.rem(s, depth)
+        return pltpu.make_async_copy(state.at[s], s_in.at[slot], in_sem.at[slot])
+
+    def store(s):
+        slot = lax.rem(s, depth)
+        return pltpu.make_async_copy(s_out.at[slot], new_state.at[s], out_sem.at[slot])
+
+    rows = [
+        pltpu.make_async_copy(source, held, load_sem.at[n])
+        for n, (source, held) in enumerate(((c_col, c_held), (k, k_held), (v, v_held)))
+    ]
+    for copy in rows:
+        copy.start()
+
+    def fill(s, carry):
+        load(s).start()
+        return carry
+
+    lax.fori_loop(0, depth, fill, 0)
+    for copy in rows:
+        copy.wait()
+
+    def step(s, carry):
+        slot = lax.rem(s, depth)
+        load(s).wait()
+
+        @pl.when(s >= depth)
+        def _():
+            store(s - depth).wait()
+
+        at = pl.ds(pl.multiple_of(s * NEW, NEW), NEW)
         for g in range(groups):
             vs = slice(g * vw, (g + 1) * vw)
-            col = c_col[at, g : g + 1]
+            col = c_held[at, g : g + 1]
             last = col[NEW - 1 : NEW, :]
-            key = k[at, g * HEAD : (g + 1) * HEAD].astype(jnp.float32)
+            key = k_held[at, g * HEAD : (g + 1) * HEAD].astype(jnp.float32)
             scaled = (key * jnp.exp(last - col)).astype(jnp.bfloat16)
             fresh = lax.dot_general(
-                scaled, v[at, vs], (((0,), (0,)), ((), ())), preferred_element_type=jnp.float32
+                scaled,
+                v_held[at, vs],
+                (((0,), (0,)), ((), ())),
+                preferred_element_type=jnp.float32,
             )
-            new_state[s, :, vs] = jnp.exp(last) * state[s, :, vs] + fresh
-
-
-def update_state(c_col, k, v, state):
-    rows, groups = c_col.shape
-    sequences = rows // NEW
-    per_step = PER_STEP if sequences % PER_STEP == 0 else 1
-    by_row = lambda width: pl.BlockSpec((per_step * NEW, width), lambda i: (i, 0))
-    state_spec = pl.BlockSpec((per_step,) + state.shape[1:], lambda i: (i, 0, 0))
+            s_out[slot, :, vs] = jnp.exp(last) * s_in[slot, :, vs] + fresh
+        store(s).start()
+
+        @pl.when(s + depth < sequences)
+        def _():
+            load(s + depth).start()
+
+        return carry
+
+    lax.fori_loop(0, sequences, step, 0)
+
+    def drain(s, carry):
+        store(sequences - depth + s).wait()
+        return carry
+
+    lax.fori_loop(0, depth, drain, 0)
+
+
+def update_state(groups, c_col, k, v, state):
+    rows = c_col.shape[0]
+    depth = min(DEPTH, state.shape[0])
+    anywhere = pl.BlockSpec(memory_space=pl.ANY)
     return pl.pallas_call(
-        functools.partial(update_step, per_step, groups),
-        grid=(sequences // per_step,),
-        in_specs=[by_row(groups), by_row(k.shape[1]), by_row(v.shape[1]), state_spec],
-        out_specs=state_spec,
+        functools.partial(update_kernel, groups),
+        in_specs=[anywhere] * 4,
+        out_specs=anywhere,
         out_shape=jax.ShapeDtypeStruct(state.shape, jnp.float32),
-        compiler_params=pltpu.CompilerParams(
-            dimension_semantics=("arbitrary",), vmem_limit_bytes=60 << 20
-        ),
+        scratch_shapes=[
+            pltpu.VMEM(c_col.shape, jnp.float32),
+            pltpu.VMEM(k.shape, k.dtype),
+            pltpu.VMEM(v.shape, v.dtype),
+            pltpu.VMEM((depth,) + state.shape[1:], jnp.float32),
+            pltpu.VMEM((depth,) + state.shape[1:], jnp.float32),
+            pltpu.SemaphoreType.DMA((3,)),
+            pltpu.SemaphoreType.DMA((depth,)),
+            pltpu.SemaphoreType.DMA((depth,)),
+        ],
+        compiler_params=pltpu.CompilerParams(vmem_limit_bytes=60 << 20),
         cost_estimate=pl.CostEstimate(
             flops=2 * rows * HEAD * v.shape[1],
             bytes_accessed=8 * state.size,
@@ -611,17 +717,8 @@
 
 
 def whole_heads(tokens, decay, state, w_query, w_key, w_value, w_gate, w_out, norm_gain):
-    tok_rows = tokens.shape[0]
     groups = w_query.shape[1] // HEAD
-    sequences = tok_rows // NEW
-    first_head = lax.axis_index("mp") * groups
-    logs = jnp.log(lax.dynamic_slice_in_dim(decay, first_head, groups, 1))
-    logs = logs.reshape(sequences, NEW, groups)
-    causal = jnp.arange(NEW)[:, None] >= jnp.arange(NEW)[None, :]
-    cumul = jnp.sum(jnp.where(causal[None, :, :, None], logs[:, None], 0.0), axis=2)
-    c_col = cumul.reshape(tok_rows, groups)
-    c_row = jnp.transpose(cumul.reshape(CHUNKS, tok_rows // CHUNKS, groups), (0, 2, 1))
-    key_proj, value_proj, reduced, own, *shares = fused(
+    key_proj, value_proj, cumul, reduced, own, *shares = fused(
         tokens,
         w_query,
         w_key,
@@ -629,8 +726,7 @@
         w_gate,
         w_out,
         state,
-        c_col,
-        c_row,
+        decay.T,
         norm_gain.reshape(1, -1),
     )
     devices = range(lax.axis_size("mp"))
@@ -638,7 +734,7 @@
         pairs = [(device, partners(device)[n]) for device in devices]
         own = own + lax.ppermute(share, "mp", pairs).astype(jnp.float32)
     layer_out = jnp.concatenate([reduced, own.astype(jnp.bfloat16)])
-    return (layer_out, update_state(c_col, key_proj, value_proj, state))
+    return (layer_out, update_state(groups, cumul, key_proj, value_proj, state))
 
 
 def per_device(tokens, decay, state, w_query, *rest):

time: 129 us -> 105 us (0.81)
  Pallas kernels: 120 us -> 99.9 us
  local copies, waits for them, and re-layouts: 2.64 us -> 0.58 us
    pallas_call x1, Pallas kernels: 88.5 us -> 76.1 us  [fused(): pl.pallas_call(functools.partial(fused_kernel, chunks, reduced, groups),...]
    pallas_call x1, Pallas kernels: 31.2 us -> 23.8 us  [update_state(): pl.pallas_call(functools.partial(update_kernel, groups), in_specs=[anywhe...]
    ppermute x3 -> x2, starting transfers between devices: 3.55 us -> 2.28 us  [whole_heads(): own = own + lax.ppermute(share, 'mp', pairs).astype(jnp.float32)]
  transfers between devices with their start and end apart: 3 -> 2, of which waited for: 0 -> 0; matrix products, arithmetic and copies ran while one was open for 0% -> 0% of each run, Pallas kernels for 24% -> 23%
where the time goes in v2:
time: 105 us
  Pallas kernels  99.9 us (95%)
  starting transfers between devices  2.28 us (2%)
  other arithmetic  1.36 us (1%)
    pallas_call x1, Pallas kernels, fused(): pl.pallas_call(functools.partial(fused_kernel, chunks, reduced, groups),...  76.1 us
    pallas_call x1, Pallas kernels, update_state(): pl.pallas_call(functools.partial(update_kernel, groups), in_specs=[anywhe...  23.8 us
    ppermute x2, starting transfers between devices, whole_heads(): own = own + lax.ppermute(share, 'mp', pairs).astype(jnp.float32)  2.28 us
  transfers between devices with their start and end apart: 2, of which 0 were waited for; matrix products, arithmetic and copies ran while one was open for 0% of the time, Pallas kernels for 23%

profile of v2, /device:TPU:0, one launch (start us, length us, event | category | flops | bytes accessed | tf_op | source)
XLA Modules:
  0.0 104.8 jit_solution(14538696125375047724)
XLA Ops:
  0.6 76.1 %shard_map.104 = (bf16[1024,512]{1,0:T(8,128)(2,1)}, bf16[1024,1024]{1,0:T(8,128)(2,1)}, f32[1024,8]{1,0:T(8,128)}, bf16[256,512]{1,0:T(8,128)(2,1)}, f32[768,51...) custom-call(bf16[1024,512]{1,0:T(8,128)(2,1)} %tokens.1, bf16[4096,512]{1,0:T(8,128)(2,1)} %w_query.1, ...), custom_call_target="tpu_custom_call" | custom-call | flops 34359738368 | bytes 33554432 | tf_op jit(solution)/shard_map/pallas_call | solution.py:561
  76.8 1.4 %collective-permute-start = (bf16[768,512]{1,0:T(8,128)(2,1)}, bf16[768,512]{1,0:T(8,128)(2,1)S(1)}, u32[]{:S(2)}, u32[]{:S(2)}) collective-permute-start(bf16[768,512]{1,0:T(8,128)(2,1)} %get-tuple-element.11), channel_id=1, source_target_pairs={{0,2},{1,5},{2,0},{3,7},{4,6},{5,1},{6,4},{7,3},{8,10},{9,13},{10,... | collective-permute-start | bytes 2359304 | tf_op jit(solution)/shard_map/ppermute | solution.py:735
  78.2 0.9 collective-permute-start.1
  79.1 0.0 copy-start
  79.1 23.8 %shard_map.105 = f32[32,256,1024]{2,1,0:T(8,128)} custom-call(f32[1024,8]{1,0:T(8,128)} %get-tuple-element.13.c_col, bf16[1024,512]{1,0:T(8,128)(2,1)} %get-tuple-element.14.k, bf16[1024,1024]{1,0:T(8,128)(2,1)} %get-tuple-element.15.v, f32[32,256,1024]{2,1,0:T(8,128)} %state.3), custom_call_target="tpu_custom_call" | custom-call | flops 536870912 | bytes 67108864 | tf_op jit(solution)/shard_map/pallas_call | solution.py:695
  102.8 0.0 copy-start.1
  102.9 0.0 collective-permute-done
  102.9 0.0 collective-permute-done.1
  102.9 0.0 copy-done
  102.9 0.3 add_convert_fusion
  103.2 0.6 copy-done.1
  103.8 1.0 pad_maximum_fusion
Async XLA Ops:
  76.8 26.1 %collective-permute-start = (bf16[768,512]{1,0:T(8,128)(2,1)}, bf16[768,512]{1,0:T(8,128)(2,1)S(1)}, u32[]{:S(2)}, u32[]{:S(2)}) collective-permute-start(bf16[768,512]{1,0:T(8,128)(2,1)} %get-tuple-element.11), channel_id=1, source_target_pairs={{0,2},{1,5},{2,0},{3,7},{4,6},{5,1},{6,4},{7,3},{8,10},{9,13},{10,... | collective-permute-start | bytes 2359304 | tf_op jit(solution)/shard_map/ppermute | solution.py:735
  78.2 24.7 %collective-permute-start.1 = (bf16[768,512]{1,0:T(8,128)(2,1)}, bf16[768,512]{1,0:T(8,128)(2,1)S(1)}, u32[]{:S(2)}, u32[]{:S(2)}) collective-permute-start(bf16[768,512]{1,0:T(8,128)(2,1)} %get-tuple-element.12), channel_id=1, source_target_pairs={{0,4},{1,3},{2,6},{3,1},{4,0},{5,7},{6,2},{7,5},{8,12},{9,11},{10,... | collective-permute-start | bytes 2359304 | tf_op jit(solution)/shard_map/ppermute | solution.py:735
  79.1 23.8 %copy-start = (f32[768,512]{1,0:T(8,128)S(1)}, f32[768,512]{1,0:T(8,128)}, u32[]{:S(2)}) copy-start(f32[768,512]{1,0:T(8,128)} %get-tuple-element.10) | copy-start | bytes 4718596
  102.8 1.0 copy-start.1

commit v3 on v2

--- a/solution.py
+++ b/solution.py
@@ -109,7 +109,6 @@
 
 
 CHUNKS = 8
-EXCHANGED = 2
 TILE = 512
 DEPTH = 8
 
@@ -145,7 +144,6 @@
 
 def fused_kernel(
     chunks,
-    reduced,
     groups,
     tokens,
     w_query,
@@ -159,7 +157,6 @@
     key_out,
     value_out,
     decay_out,
-    layer_out,
     own_out,
     near_out,
     far_out,
@@ -182,7 +179,6 @@
     total,
     parts,
     pending,
-    finished,
     cumul,
     cumul_row,
     load_sem,
@@ -223,13 +219,13 @@
             sibling,
         )
 
-    def hop(lane, r):
+    def hop(r):
         return remote(
-            outgoing.at[lane, at(r), :],
-            incoming.at[lane, at(r), :],
-            sum_send.at[4 + lane, r],
-            sum_recv.at[4 + lane, r],
-            near if lane == 0 else far,
+            outgoing.at[2, at(r), :],
+            incoming.at[at(r), :],
+            sum_send.at[4, r],
+            sum_recv.at[4, r],
+            far,
         )
 
     own = pltpu.make_async_copy(tokens, gathered.at[:, span(me)], load_sem.at[0])
@@ -259,18 +255,12 @@
             v_held.at[lax.rem(r, 2)], value_out.at[at(r), :], kv_sem.at[1, r]
         )
 
-    def store_layer(r):
-        return pltpu.make_async_copy(
-            finished.at[at(r), :], layer_out.at[at(r), :], out_sem.at[0, r]
-        )
-
     def store_shares(r):
-        there = at(r - reduced)
-        return [pltpu.make_async_copy(total.at[at(r), :], own_out.at[there, :], out_sem.at[0, r])] + [
-            pltpu.make_async_copy(
-                outgoing.at[lane, at(r), :], target.at[there, :], out_sem.at[1 + lane, r]
+        return [
+            pltpu.make_async_copy(source.at[at(r), :], target.at[at(r), :], out_sem.at[n, r])
+            for n, (source, target) in enumerate(
+                ((total, own_out), (outgoing.at[0], near_out), (outgoing.at[1], far_out))
             )
-            for lane, target in enumerate((near_out, far_out))
         ]
 
     meet((near, far, sibling))
@@ -349,49 +339,23 @@
             part = parts[slot, j] + from_sibling[j, at(r), :].astype(jnp.float32)
             if j >= 2:
                 outgoing[j - 1, at(r), :] = part.astype(jnp.bfloat16)
+                if j == 3:
+                    hop(r).start()
             elif j == 1:
                 pending[slot] = part
             else:
                 total[at(r), :] = part
-        hop(2, r).start()
-
-        @pl.when(r < reduced)
-        def _():
-            hop(1, r).start()
 
     def relay(r):
-        hop(2, r).wait_recv()
-        part = pending[lax.rem(r, 2)] + incoming[2, at(r), :].astype(jnp.float32)
+        hop(r).wait_recv()
+        part = pending[lax.rem(r, 2)] + incoming[at(r), :].astype(jnp.float32)
         outgoing[0, at(r), :] = part.astype(jnp.bfloat16)
-
-        @pl.when(r < reduced)
-        def _():
-            hop(0, r).start()
-
-        @pl.when(r >= reduced)
-        def _():
-            for store in store_shares(r):
-                store.start()
-
-    def finish(r):
-        hop(1, r).wait_recv()
-        hop(0, r).wait_recv()
-        finished[at(r), :] = (
-            total[at(r), :]
-            + incoming[0, at(r), :].astype(jnp.float32)
-            + incoming[1, at(r), :].astype(jnp.float32)
-        ).astype(jnp.bfloat16)
-        store_layer(r).start()
+        for store in store_shares(r):
+            store.start()
 
     def step(r, carry):
         slot = lax.rem(r, 2)
         load_state(r).start()
-
-        @pl.when(r + 4 < chunks)
-        def _():
-            copy(0, me, near, r + 4).start()
-            give_far(r + 4)
-
         for lane, source in ((3, sibling), (4, sib_near), (5, sib_far), (6, sib_diagonal)):
             copy(lane, source, sibling, r).wait_recv()
 
@@ -422,11 +386,19 @@
         store_key(r).start()
         store_value(r).start()
 
-        @pl.when(r == 0)
-        def _():
-            pass_diagonal(1)
-            pass_near(2)
-            pass_far(2)
+        @pl.when(r + 1 < chunks)
+        def _():
+            pass_diagonal(r + 1)
+
+        @pl.when(r + 2 < chunks)
+        def _():
+            pass_near(r + 2)
+            pass_far(r + 2)
+
+        @pl.when(r + 4 < chunks)
+        def _():
+            copy(0, me, near, r + 4).start()
+            give_far(r + 4)
 
         @pl.when(r >= 2)
         def _():
@@ -435,10 +407,6 @@
         @pl.when(r >= 1)
         def _():
             combine(r - 1)
-
-        @pl.when((r >= 4) & (r - 4 < reduced))
-        def _():
-            finish(r - 4)
 
         load_state(r).wait()
         for g in range(groups):
@@ -478,23 +446,12 @@
         for j in (3, 2, 1, 0):
             swap(j, r).start()
 
-        @pl.when(r + 2 < chunks)
-        def _():
-            pass_diagonal(r + 2)
-
-        @pl.when(r + 3 < chunks)
-        def _():
-            pass_near(r + 3)
-            pass_far(r + 3)
-
         return carry
 
     lax.fori_loop(0, chunks, step, 0)
     combine(chunks - 1)
     relay(chunks - 2)
     relay(chunks - 1)
-    for r in range(chunks - 4, reduced):
-        finish(r)
     decay_copy.wait()
 
     def drain(r, carry):
@@ -518,19 +475,9 @@
             for j in range(4):
                 swap(j, r).wait_send()
 
-        hop(2, r).wait_send()
-
-        @pl.when(r < reduced)
-        def _():
-            for lane in range(2):
-                hop(lane, r).wait_send()
-            store_layer(r).wait()
-
-        @pl.when(r >= reduced)
-        def _():
-            for store in store_shares(r):
-                store.wait()
-
+        hop(r).wait_send()
+        for store in store_shares(r):
+            store.wait()
         return carry
 
     lax.fori_loop(0, chunks, drain, 0)
@@ -540,11 +487,9 @@
     rows, width = tokens.shape
     depth, qk = w_query.shape
     vc = w_value.shape[1]
-    chunks, reduced = CHUNKS, EXCHANGED
+    chunks = CHUNKS
     size = rows // chunks
     groups = qk // HEAD
-    kept = reduced * size
-    rest = rows - kept
     anywhere = pl.BlockSpec(memory_space=pl.ANY)
     vmem = pl.BlockSpec(memory_space=pltpu.VMEM)
     narrow = jnp.bfloat16
@@ -553,13 +498,12 @@
         ((rows, qk), narrow),
         ((rows, vc), narrow),
         ((rows, 8), wide),
-        ((kept, width), narrow),
-        ((rest, width), wide),
-        ((rest, width), narrow),
-        ((rest, width), narrow),
+        ((rows, width), wide),
+        ((rows, width), narrow),
+        ((rows, width), narrow),
     ]
     return pl.pallas_call(
-        functools.partial(fused_kernel, chunks, reduced, groups),
+        functools.partial(fused_kernel, chunks, groups),
         in_specs=[anywhere] * 7 + [vmem] * 2,
         out_specs=[anywhere] * len(shapes),
         out_shape=[jax.ShapeDtypeStruct(*shape) for shape in shapes],
@@ -579,21 +523,20 @@
             pltpu.VMEM((2, 4, size, width), narrow),
             pltpu.VMEM((4, rows, width), narrow),
             pltpu.VMEM((3, rows, width), narrow),
-            pltpu.VMEM((3, rows, width), narrow),
+            pltpu.VMEM((rows, width), narrow),
             pltpu.VMEM((rows, width), wide),
             pltpu.VMEM((2, 4, size, width), wide),
             pltpu.VMEM((2, size, width), wide),
-            pltpu.VMEM((kept, width), narrow),
             pltpu.VMEM((rows, 8), wide),
             pltpu.VMEM((chunks, 8, size), wide),
             pltpu.SemaphoreType.DMA((7,)),
             pltpu.SemaphoreType.DMA((1,)),
             pltpu.SemaphoreType.DMA((2, chunks)),
-            pltpu.SemaphoreType.DMA((4, chunks)),
+            pltpu.SemaphoreType.DMA((3, chunks)),
             pltpu.SemaphoreType.DMA((7, chunks)),
             pltpu.SemaphoreType.DMA((7, chunks)),
-            pltpu.SemaphoreType.DMA((7, chunks)),
-            pltpu.SemaphoreType.DMA((7, chunks)),
+            pltpu.SemaphoreType.DMA((5, chunks)),
+            pltpu.SemaphoreType.DMA((5, chunks)),
         ],
         compiler_params=pltpu.CompilerParams(
             collective_id=0, has_side_effects=True, vmem_limit_bytes=67043328
@@ -718,7 +661,7 @@
 
 def whole_heads(tokens, decay, state, w_query, w_key, w_value, w_gate, w_out, norm_gain):
     groups = w_query.shape[1] // HEAD
-    key_proj, value_proj, cumul, reduced, own, *shares = fused(
+    key_proj, value_proj, cumul, own, *shares = fused(
         tokens,
         w_query,
         w_key,
@@ -733,8 +676,7 @@
     for n, share in enumerate(shares):
         pairs = [(device, partners(device)[n]) for device in devices]
         own = own + lax.ppermute(share, "mp", pairs).astype(jnp.float32)
-    layer_out = jnp.concatenate([reduced, own.astype(jnp.bfloat16)])
-    return (layer_out, update_state(groups, cumul, key_proj, value_proj, state))
+    return (own.astype(jnp.bfloat16), update_state(groups, cumul, key_proj, value_proj, state))
 
 
 def per_device(tokens, decay, state, w_query, *rest):

time: 105 us -> 102 us (0.971)
  Pallas kernels: 99.9 us -> 95.9 us
  other arithmetic: 1.36 us -> 2.62 us
    pallas_call x1, Pallas kernels: 76.1 us -> 72.1 us  [fused(): pl.pallas_call(functools.partial(fused_kernel, chunks, groups), in_specs=...]
    convert_element_type x1, other arithmetic: 0.32 us -> 2.62 us  [whole_heads(): own.astype(jnp.bfloat16)]
where the time goes in v3:
time: 102 us; the launch traced here: 101 us
  Pallas kernels  95.9 us (94%)
  other arithmetic  2.62 us (3%)
  starting transfers between devices  2.09 us (2%)
    pallas_call x1, Pallas kernels, fused(): pl.pallas_call(functools.partial(fused_kernel, chunks, groups), in_specs=...  72.1 us
    pallas_call x1, Pallas kernels, update_state(): pl.pallas_call(functools.partial(update_kernel, groups), in_specs=[anywhe...  23.8 us
    convert_element_type x1, other arithmetic, whole_heads(): own.astype(jnp.bfloat16)  2.62 us
    ppermute x2, starting transfers between devices, whole_heads(): own = own + lax.ppermute(share, 'mp', pairs).astype(jnp.float32)  2.09 us
  transfers between devices with their start and end apart: 2, of which 0 were waited for; matrix products, arithmetic and copies ran while one was open for 0% of the time, Pallas kernels for 23%

profile of v3, /device:TPU:0, one launch (start us, length us, event | category | flops | bytes accessed | tf_op | source)
XLA Modules:
  0.0 101.3 jit_solution(18407651760494116986)
XLA Ops:
  0.6 72.1 %shard_map.104 = (bf16[1024,512]{1,0:T(8,128)(2,1)}, bf16[1024,1024]{1,0:T(8,128)(2,1)}, f32[1024,8]{1,0:T(8,128)}, f32[1024,512]{1,0:T(8,128)}, bf16[1024,512]{1,0:T(8,128)(2,1)}, /*index=5*/bf16[1024,512]{1,0:T(8,128)(2,1)}) custom-call(bf16[1024,512]{1,0:T(8,128)(2,1)} %tokens.1, bf16[4096,512]{1,0:T(8,128)(2,1)} %w_query.1, bf16[4096,512]{1,0:T(8,128)(2,1)} %w_key.1, ...), custom_call_target="tpu_custom_call" | custom-call | flops 34359738368 | bytes 33554432 | tf_op jit(solution)/shard_map/pallas_call | solution.py:505
  72.7 0.5 collective-permute-start
  73.2 1.6 %collective-permute-start.1 = (bf16[1024,512]{1,0:T(8,128)(2,1)}, bf16[1024,512]{1,0:T(8,128)(2,1)}, u32[]{:S(2)}, u32[]{:S(2)}) collective-permute-start(bf16[1024,512]{1,0:T(8,128)(2,1)} %get-tuple-element.10), channel_id=1, source_target_pairs={{0,4},{1,3},{2,6},{3,1},{4,0},{5,7},{6,2},{7,5},{8,12},{9,11},{10,... | collective-permute-start | bytes 3145736 | tf_op jit(solution)/shard_map/ppermute | solution.py:678
  74.8 0.0 copy-start
  74.8 23.8 %shard_map.105 = f32[32,256,1024]{2,1,0:T(8,128)} custom-call(f32[1024,8]{1,0:T(8,128)} %get-tuple-element.11.c_col, bf16[1024,512]{1,0:T(8,128)(2,1)} %get-tuple-element.12.k, bf16[1024,1024]{1,0:T(8,128)(2,1)} %get-tuple-element.13.v, f32[32,256,1024]{2,1,0:T(8,128)} %state.3), custom_call_target="tpu_custom_call" | custom-call | flops 536870912 | bytes 67108864 | tf_op jit(solution)/shard_map/pallas_call | solution.py:638
  98.6 0.0 collective-permute-done
  98.6 0.0 collective-permute-done.1
  98.6 0.1 copy-done
  98.7 2.6 %add_convert_fusion = bf16[1024,512]{1,0:T(8,128)(2,1)} fusion(bf16[1024,512]{1,0:T(8,128)(2,1)} %collective-permute-done.1, f32[1024,512]{1,0:T(8,128)S(1)} %copy-done, bf16[1024,512]{1,0:T(8,128)(2,1)S(1)} %collective-permute-done), kind=kLoop, calls=%fused_computation | loop fusion | flops 2621440 | bytes 5242880 | tf_op jit(solution)/shard_map/convert_element_type | solution.py:679
Async XLA Ops:
  72.7 25.9 %collective-permute-start = (bf16[1024,512]{1,0:T(8,128)(2,1)}, bf16[1024,512]{1,0:T(8,128)(2,1)S(1)}, u32[]{:S(2)}, u32[]{:S(2)}) collective-permute-start(bf16[1024,512]{1,0:T(8,128)(2,1)} %get-tuple-element.9), channel_id=1, source_target_pairs={{0,2},{1,5},{2,0},{3,7},{4,6},{5,1},{6,4},{7,3},{8,10},{9,13},{10,... | collective-permute-start | bytes 3145736 | tf_op jit(solution)/shard_map/ppermute | solution.py:678
  73.2 25.4 %collective-permute-start.1 = (bf16[1024,512]{1,0:T(8,128)(2,1)}, bf16[1024,512]{1,0:T(8,128)(2,1)}, u32[]{:S(2)}, u32[]{:S(2)}) collective-permute-start(bf16[1024,512]{1,0:T(8,128)(2,1)} %get-tuple-element.10), channel_id=1, source_target_pairs={{0,4},{1,3},{2,6},{3,1},{4,0},{5,7},{6,2},{7,5},{8,12},{9,11},{10,... | collective-permute-start | bytes 3145736 | tf_op jit(solution)/shard_map/ppermute | solution.py:678
  74.8 23.9 %copy-start = (f32[1024,512]{1,0:T(8,128)S(1)}, f32[1024,512]{1,0:T(8,128)}, u32[]{:S(2)}) copy-start(f32[1024,512]{1,0:T(8,128)} %get-tuple-element.8) | copy-start | bytes 6291460
